TPU v7x, 256 devices: a whole 4x4x8 slice. The times are simulated.
256 devices in a mesh: atom: 32 (over y_lo, z, core), band: 8 (over y_hi, x).
Axes of the slice: x: 4, y: 4 (y_hi: 2, y_lo: 2; y = y_hi * 2 + y_lo), z: 8, core: 2. Of those that a mesh axis runs over, the one named last changes fastest.
Arguments:
- wave_rows: bfloat16 [512, 65536], P('atom', 'band'), may hold values from -6 to 6
- projectors: bfloat16 [4096, 65536], P('atom', 'band'), may hold values from -0.0234375 to 0.0234375
- dij_table: float32 [16, 8, 8], replicated, may hold values from -6 to 6
- dij_index: int32 [512], P('atom'), may hold values from 0 to 15
- proj_count: int32 [512], P('atom'), may hold values from 1 to 8
Outputs:
- nonlocal_rows: bfloat16 [512, 65536], P('atom', 'band')
All inputs are finite; a program needn't handle non-finite values.
Results may differ from a plain program's by a relative error of at most 0.0049.
Values may be sent and summed in bfloat16 or wider, within the bound.
A program may use at most 128 MiB of HBM per device.

v0:
```python
import jax
import jax.numpy as jnp
from jax import lax
from jax.sharding import Mesh
from jax.sharding import PartitionSpec as P

ATOM = ("atom_0", "atom_1", "atom_2")


def cut_along(shard, dim, count):
    before, after = (shard.shape[:dim], shard.shape[dim + 1 :])
    return jnp.moveaxis(shard.reshape(*before, count, -1, *after), dim, 0)


def sum_at_owner(shard, axis, dim):
    count = lax.axis_size(axis)
    blocks = lax.all_to_all(cut_along(shard, dim, count), axis, 0, 0, tiled=True)
    return jnp.sum(blocks, axis=0)


def sent_to_all(shard, axis):
    count = lax.axis_size(axis)
    return lax.all_to_all(
        jnp.broadcast_to(shard[None], (count, *shard.shape)), axis, 0, 0, tiled=True
    )


def in_order(blocks, dim):
    blocks = jnp.moveaxis(blocks, 0, dim)
    lengths = blocks.shape
    return blocks.reshape(*lengths[:dim], lengths[dim] * lengths[dim + 1], *lengths[dim + 2 :])


def gathered_copies(shard, axis, dim):
    blocks = sent_to_all(shard, axis)
    return in_order(blocks, dim)


def scatter_pairs(shard, chips, core, dim):
    sizes = (lax.axis_size(chips), lax.axis_size(core))
    blocks = cut_along(shard, dim, sizes[0] * sizes[1])
    inside = blocks.shape[1:]
    blocks = blocks.reshape(*sizes, *inside).swapaxes(0, 1).reshape(-1, *inside)
    blocks = lax.psum_scatter(blocks, core, scatter_dimension=0, tiled=True)
    return lax.psum_scatter(blocks, chips, scatter_dimension=0, tiled=True)[0]


def shards(wave_rows, projectors, dij_table, dij_index, proj_count):
    atom_local = dij_index.shape[0]
    kind_total = dij_table.shape[0]
    per_atom = dij_table.shape[1]
    width = atom_local * per_atom
    partial_value = lax.dot_general(
        lax.all_gather(wave_rows, ATOM, axis=0, tiled=True),
        projectors,
        (((1,), (1,)), ((), ())),
        preferred_element_type=jnp.float32,
    )
    kind_onehot = (dij_index[:, None] == jnp.arange(kind_total, dtype=jnp.int32)[None, :]).astype(
        jnp.float32
    )
    blocks = jnp.dot(
        kind_onehot,
        dij_table.reshape(kind_total, per_atom * per_atom),
        precision=lax.Precision.HIGHEST,
    ).reshape(atom_local, per_atom, per_atom)
    active = (jnp.arange(per_atom, dtype=jnp.int32)[None, :] < proj_count[:, None]).astype(
        jnp.float32
    )
    blocks = blocks * active[:, :, None] * active[:, None, :]
    share = sum_at_owner(partial_value, "band", 0)
    count = share.shape[0]
    mixed = jnp.einsum(
        "baj,aij->bai",
        share.reshape(count, atom_local, per_atom),
        blocks,
        precision=lax.Precision.HIGHEST,
    )
    weighted = gathered_copies(mixed.reshape(count, width).astype(jnp.bfloat16), "band", 0)
    result = scatter_pairs(
        jnp.dot(weighted, projectors, preferred_element_type=jnp.float32),
        ("atom_0", "atom_1"),
        "atom_2",
        0,
    )
    return result.astype(jnp.bfloat16)


def solution(mesh):
    split = Mesh(
        mesh.devices.reshape(2, 8, 2, mesh.shape["band"]), ("atom_0", "atom_1", "atom_2", "band")
    )
    return jax.shard_map(
        shards,
        mesh=split,
        in_specs=(P(ATOM, "band"), P(ATOM, "band"), P(), P(ATOM), P(ATOM)),
        out_specs=P(ATOM, "band"),
        check_vma=False,
    )
```

profile of v0, /device:TPU:1, one launch (start us, length us, event | category | flops | bytes accessed | tf_op | source)
XLA Modules:
  0.0 265.8 jit_solution(16585991134371336601)
XLA Ops:
  6.5 0.0 copy-start
  6.5 0.0 copy-start.3
  6.5 0.0 copy-start.2
  6.5 0.0 copy-start.1
  6.5 0.0 all-gather.2.cloned.1.call-start
  6.6 0.7 all-gather.2.cloned.1.call-update
  7.3 77.8 %all-gather.2.cloned.1.call-done = bf16[512,8192]{1,0:T(8,128)(2,1)} async-done(((bf16[16,8192]{1,0:T(8,128)(2,1)}), bf16[512,8192]{1,0:T(8,128)(2,1)}) %all-gather.2.cloned.1.call-update) | async-done | bytes 8388624 | tf_op jit(solution)/shard_map/all_gather | solution.py:54
  85.1 0.0 copy-done
  85.1 6.4 %fusion.9 = f32[512,128]{1,0:T(8,128)} fusion(bf16[512,8192]{1,0:T(8,128)(2,1)} %all-gather.2.cloned.1.call-done, bf16[128,8192]{1,0:T(8,128)(2,1)S(1)} %copy-done), kind=kOutput, calls=%fused_computation.14 | convolution fusion | flops 1073741824 | bytes 10747904 | tf_op jit(solution)/shard_map/dot_general | solution.py:53
  91.5 6.5 %all-to-all-start = ((f32[8,64,128]{2,1,0:T(8,128)}), f32[8,64,128]{2,1,0:T(8,128)S(1)}, u32[]{:S(2)}, u32[]{:S(2)}) async-start(f32[8,64,128]{2,1,0:T(8,128)} %bitcast.4), calls=%async_computation | async-start | bytes 524288 | tf_op jit(solution)/shard_map/all_to_all | solution.py:17
  98.0 0.0 reduce-scatter.3.cloned.1.call-start
  98.0 0.0 copy-done.3
  98.1 0.0 copy-done.2
  98.1 0.0 copy-done.1
  98.1 0.2 fusion.2
  98.3 0.1 copy.14
  98.4 8.5 %all-to-all-done = f32[8,64,128]{2,1,0:T(8,128)S(1)} async-done(((f32[8,64,128]{2,1,0:T(8,128)}), f32[8,64,128]{2,1,0:T(8,128)S(1)}, u32[]{:S(2)}, u32[]{:S(2)}) %all-to-all-start) | async-done | bytes 262176 | tf_op jit(solution)/shard_map/all_to_all | solution.py:17
  106.9 0.1 copy.13
  107.0 0.3 fusion.1
  107.3 0.1 copy.15
  107.4 9.3 %all_to_all.10 = bf16[8,64,128]{2,1,0:T(8,128)(2,1)S(1)} all-to-all(bf16[8,64,128]{2,1,0:T(8,128)(2,1)S(1)} %broadcast_in_dim.2), channel_id=1, replica_groups=mesh['atom_0'=2,'atom_1'=8,'atom_2'=2,'band'=8] {'band'}, dimensions={0} | all-to-all | bytes 262144 | tf_op jit(solution)/shard_map/all_to_all | solution.py:23
  116.8 2.3 convolution_bitcast_fusion
  119.1 6.0 %copy.16 = f32[2,16,16,8192]{3,2,1,0:T(8,128)} copy(f32[2,16,16,8192]{3,2,0,1:T(8,128)S(1)} %convolution_bitcast_fusion) | data formatting | bytes 33554432 | tf_op jit(solution)/shard_map/transpose | solution.py:43
  125.2 0.0 reduce-scatter.3.cloned.1.call-update
  125.2 0.0 reduce-scatter.5.cloned.1.call-start
  125.2 27.9 %reduce-scatter.3.cloned.1.call-done = f32[16,16,8192]{2,1,0:T(8,128)} async-done(((f32[32,16,8192]{2,1,0:T(8,128)}), f32[16,16,8192]{2,1,0:T(8,128)}) %reduce-scatter.3.cloned.1.call-update) | async-done | bytes 8388624 | tf_op jit(solution)/shard_map/reduce_scatter | solution.py:44
  153.1 0.0 reduce-scatter.5.cloned.1.call-update
  153.1 104.4 %reduce-scatter.5.cloned.1.call-done = f32[1,16,8192]{2,1,0:T(8,128)} async-done(((f32[16,16,8192]{2,1,0:T(8,128)}), f32[1,16,8192]{2,1,0:T(8,128)}) %reduce-scatter.5.cloned.1.call-update) | async-done | bytes 524304 | tf_op jit(solution)/shard_map/reduce_scatter | solution.py:45
  257.5 1.8 convert_bitcast_fusion
  (3 shorter events, 0.1 us)
Async XLA Ops:
  6.5 78.6 %copy-start = (bf16[128,8192]{1,0:T(8,128)(2,1)S(1)}, bf16[128,8192]{1,0:T(8,128)(2,1)}, u32[]{:S(2)}) copy-start(bf16[128,8192]{1,0:T(8,128)(2,1)} %param.6) | copy-start | bytes 6291460
  6.5 91.5 %copy-start.3 = (s32[16]{0:T(128)S(1)}, s32[16]{0:T(128)}, u32[]{:S(2)}) copy-start(s32[16]{0:T(128)} %param.9) | copy-start | bytes 196
  6.5 91.5 %copy-start.2 = (s32[16]{0:T(128)S(1)}, s32[16]{0:T(128)}, u32[]{:S(2)}) copy-start(s32[16]{0:T(128)} %param.8) | copy-start | bytes 196
  6.5 91.5 %copy-start.1 = (f32[16,8,8]{0,2,1:T(8,128)S(1)}, f32[16,8,8]{0,2,1:T(8,128)}, u32[]{:S(2)}) copy-start(f32[16,8,8]{0,2,1:T(8,128)} %param.7) | copy-start | bytes 12292
  6.5 78.6 %all-gather.2.cloned.1.call-start = ((), (), s32[]{:S(2)}) async-start(), calls=%async_computation.4 | async-start | bytes 8650752 | tf_op jit(solution)/shard_map/all_gather | solution.py:54
  91.5 15.4 %all-to-all-start = ((f32[8,64,128]{2,1,0:T(8,128)}), f32[8,64,128]{2,1,0:T(8,128)S(1)}, u32[]{:S(2)}, u32[]{:S(2)}) async-start(f32[8,64,128]{2,1,0:T(8,128)} %bitcast.4), calls=%async_computation | async-start | bytes 524288 | tf_op jit(solution)/shard_map/all_to_all | solution.py:17
  98.0 55.1 %reduce-scatter.3.cloned.1.call-start = ((), (), s32[]{:S(2)}) async-start(), calls=%async_computation.5 | async-start | bytes 25165824 | tf_op jit(solution)/shard_map/reduce_scatter | solution.py:44
  125.2 132.3 %reduce-scatter.5.cloned.1.call-start = ((), (), s32[]{:S(2)}) async-start(), calls=%async_computation.6 | async-start | bytes 8912896 | tf_op jit(solution)/shard_map/reduce_scatter | solution.py:45
Sparse Core Ops, SparseCore 0:
  9.2 75.8 all-gather.1
  125.3 27.7 reduce-scatter.2
  155.6 101.8 reduce-scatter.4
where the time goes:
time: 266 us
  waiting for transfers between devices  219 us (82%)
  between operations  13.2 us (5%)
  blocking collectives  9.35 us (4%)
  matrix products  9.21 us (3%)
  starting transfers between devices  6.58 us (2%)
  local copies, waits for them, and re-layouts  6.35 us (2%)
    reduce_scatter x1, waiting for transfers between devices, scatter_pairs(): return lax.psum_scatter(blocks, chips, scatter_dimension=0, tiled=True)[0]  104 us
    all_gather x1, waiting for transfers between devices, shards(): lax.all_gather(wave_rows, ATOM, axis=0, tiled=True)  77.8 us
    reduce_scatter x1, waiting for transfers between devices, scatter_pairs(): blocks = lax.psum_scatter(blocks, core, scatter_dimension=0, tiled=True)  27.9 us
    all_to_all x1, blocking collectives, sent_to_all(): lax.all_to_all(jnp.broadcast_to(shard[None], (count, *shard.shape)), axis...  9.35 us
    all_to_all x1, waiting for transfers between devices, sum_at_owner(): lax.all_to_all(cut_along(shard, dim, count), axis, 0, 0, tiled=True)  8.53 us
    all_to_all x1, starting transfers between devices, sum_at_owner(): lax.all_to_all(cut_along(shard, dim, count), axis, 0, 0, tiled=True)  6.47 us
    dot_general x1, matrix products, shards(): lax.dot_general(lax.all_gather(wave_rows, ATOM, axis=0, tiled=True), proj...  6.41 us
    transpose x1, local copies, waits for them, and re-layouts, scatter_pairs(): blocks = blocks.reshape(*sizes, *inside).swapaxes(0, 1).reshape(-1, *inside)  6.05 us
  transfers between devices with their start and end apart: 4, of which 4 were waited for; matrix products, arithmetic and copies ran while one was open for 0% of the time, Pallas kernels for 0%

commit v1 on v0

--- a/solution.py
+++ b/solution.py
@@ -51,7 +51,9 @@
     per_atom = dij_table.shape[1]
     width = atom_local * per_atom
     partial_value = lax.dot_general(
-        lax.all_gather(wave_rows, ATOM, axis=0, tiled=True),
+        jnp.concatenate(
+            lax.all_to_all(jnp.stack([wave_rows] * lax.axis_size(ATOM)), ATOM, 0, 0), axis=0
+        ),
         projectors,
         (((1,), (1,)), ((), ())),
         preferred_element_type=jnp.float32,

time: 266 us -> 381 us (1.43)
  blocking collectives: 9.35 us -> 204 us
  waiting for transfers between devices: 219 us -> 141 us
    all_to_all x0 -> x1, blocking collectives: none -> 195 us  [shards(): lax.all_to_all(jnp.stack([wave_rows] * lax.axis_size(ATOM)), ATOM, 0, 0)]
    all_gather x1 -> x0, waiting for transfers between devices: 77.8 us -> none  [shards(): lax.all_gather(wave_rows, ATOM, axis=0, tiled=True)]
  transfers between devices with their start and end apart: 4 -> 3, of which waited for: 4 -> 3; matrix products, arithmetic and copies ran while one was open for 0% -> 0% of each run, Pallas kernels for 0% -> 0%
where the time goes in v1:
time: 381 us
  blocking collectives  204 us (54%)
  waiting for transfers between devices  141 us (37%)
  between operations  13.5 us (4%)
  local copies, waits for them, and re-layouts  8.45 us (2%)
  starting transfers between devices  6.43 us (2%)
  matrix products  5.84 us (2%)
    all_to_all x1, blocking collectives, shards(): lax.all_to_all(jnp.stack([wave_rows] * lax.axis_size(ATOM)), ATOM, 0, 0)  195 us
    reduce_scatter x1, waiting for transfers between devices, scatter_pairs(): return lax.psum_scatter(blocks, chips, scatter_dimension=0, tiled=True)[0]  104 us
    reduce_scatter x1, waiting for transfers between devices, scatter_pairs(): blocks = lax.psum_scatter(blocks, core, scatter_dimension=0, tiled=True)  29.1 us
    all_to_all x1, blocking collectives, sent_to_all(): lax.all_to_all(jnp.broadcast_to(shard[None], (count, *shard.shape)), axis...  9.42 us
  transfers between devices with their start and end apart: 3, of which 3 were waited for; matrix products, arithmetic and copies ran while one was open for 0% of the time, Pallas kernels for 0%

profile of v1, /device:TPU:1, one launch (start us, length us, event | category | flops | bytes accessed | tf_op | source)
XLA Modules:
  0.0 381.1 jit_solution(9786906605257926729)
XLA Ops:
  6.5 0.0 copy-start
  6.5 2.1 stack.2
  8.6 194.7 %all_to_all.15 = bf16[32,16,8192]{2,1,0:T(8,128)(2,1)S(1)} all-to-all(bf16[32,16,8192]{2,1,0:T(8,128)(2,1)S(1)} %stack.2), channel_id=1, replica_groups=mesh['atom_0'=2,'atom_1'=8,'atom_2'=2,'band'=8] {'atom_0','atom_1','atom..., dimensions={0} | all-to-all | bytes 16777216 | tf_op jit(solution)/shard_map/all_to_all | solution.py:55
  203.4 0.0 copy-start.3
  203.4 0.0 copy-start.1
  203.4 0.0 copy-start.2
  203.4 0.0 copy-done
  203.4 3.0 fusion.1
  206.4 6.4 %all-to-all-start.1 = ((f32[8,64,128]{2,1,0:T(8,128)}), f32[8,64,128]{2,1,0:T(8,128)S(1)}, u32[]{:S(2)}, u32[]{:S(2)}) async-start(f32[8,64,128]{2,1,0:T(8,128)} %fusion.1), calls=%async_computation.1 | async-start | bytes 524288 | tf_op jit(solution)/shard_map/all_to_all | solution.py:17
  212.8 0.0 reduce-scatter.3.cloned.1.call-start
  212.8 0.0 copy-done.3
  212.8 0.0 copy-done.1
  212.9 0.0 copy-done.2
  212.9 0.2 fusion.4
  213.1 0.1 copy.14
  213.2 7.3 %all-to-all-done.1 = f32[8,64,128]{2,1,0:T(8,128)S(1)} async-done(((f32[8,64,128]{2,1,0:T(8,128)}), f32[8,64,128]{2,1,0:T(8,128)S(1)}, u32[]{:S(2)}, u32[]{:S(2)}) %all-to-all-start.1) | async-done | bytes 262176 | tf_op jit(solution)/shard_map/all_to_all | solution.py:17
  220.5 0.1 copy.13
  220.6 0.3 fusion.3
  220.9 0.1 copy.15
  221.0 9.4 %all_to_all.16 = bf16[8,64,128]{2,1,0:T(8,128)(2,1)S(1)} all-to-all(bf16[8,64,128]{2,1,0:T(8,128)(2,1)S(1)} %broadcast_in_dim.2), channel_id=1, replica_groups=mesh['atom_0'=2,'atom_1'=8,'atom_2'=2,'band'=8] {'band'}, dimensions={0} | all-to-all | bytes 262144 | tf_op jit(solution)/shard_map/all_to_all | solution.py:23
  230.4 2.3 convolution_bitcast_fusion
  232.7 6.0 %copy.16 = f32[2,16,16,8192]{3,2,1,0:T(8,128)} copy(f32[2,16,16,8192]{3,2,0,1:T(8,128)S(1)} %convolution_bitcast_fusion) | data formatting | bytes 33554432 | tf_op jit(solution)/shard_map/transpose | solution.py:43
  238.8 0.0 reduce-scatter.3.cloned.1.call-update
  238.8 0.0 reduce-scatter.5.cloned.1.call-start
  238.9 29.1 %reduce-scatter.3.cloned.1.call-done = f32[16,16,8192]{2,1,0:T(8,128)} async-done(((f32[32,16,8192]{2,1,0:T(8,128)}), f32[16,16,8192]{2,1,0:T(8,128)}) %reduce-scatter.3.cloned.1.call-update) | async-done | bytes 8388624 | tf_op jit(solution)/shard_map/reduce_scatter | solution.py:44
  268.0 0.0 reduce-scatter.5.cloned.1.call-update
  268.0 104.4 %reduce-scatter.5.cloned.1.call-done = f32[1,16,8192]{2,1,0:T(8,128)} async-done(((f32[16,16,8192]{2,1,0:T(8,128)}), f32[1,16,8192]{2,1,0:T(8,128)}) %reduce-scatter.5.cloned.1.call-update) | async-done | bytes 524304 | tf_op jit(solution)/shard_map/reduce_scatter | solution.py:45
  372.5 1.8 convert_bitcast_fusion
  (3 shorter events, 0.1 us)
Async XLA Ops:
  6.5 196.9 %copy-start = (bf16[128,8192]{1,0:T(8,128)(2,1)S(1)}, bf16[128,8192]{1,0:T(8,128)(2,1)}, u32[]{:S(2)}) copy-start(bf16[128,8192]{1,0:T(8,128)(2,1)} %param.6) | copy-start | bytes 6291460
  203.4 9.4 %copy-start.3 = (s32[16]{0:T(128)S(1)}, s32[16]{0:T(128)}, u32[]{:S(2)}) copy-start(s32[16]{0:T(128)} %param.9) | copy-start | bytes 196
  203.4 9.5 %copy-start.1 = (f32[16,8,8]{0,2,1:T(8,128)S(1)}, f32[16,8,8]{0,2,1:T(8,128)}, u32[]{:S(2)}) copy-start(f32[16,8,8]{0,2,1:T(8,128)} %param.7) | copy-start | bytes 12292
  203.4 9.5 %copy-start.2 = (s32[16]{0:T(128)S(1)}, s32[16]{0:T(128)}, u32[]{:S(2)}) copy-start(s32[16]{0:T(128)} %param.8) | copy-start | bytes 196
  206.4 14.1 %all-to-all-start.1 = ((f32[8,64,128]{2,1,0:T(8,128)}), f32[8,64,128]{2,1,0:T(8,128)S(1)}, u32[]{:S(2)}, u32[]{:S(2)}) async-start(f32[8,64,128]{2,1,0:T(8,128)} %fusion.1), calls=%async_computation.1 | async-start | bytes 524288 | tf_op jit(solution)/shard_map/all_to_all | solution.py:17
  212.8 55.2 %reduce-scatter.3.cloned.1.call-start = ((), (), s32[]{:S(2)}) async-start(), calls=%async_computation.5 | async-start | bytes 25165824 | tf_op jit(solution)/shard_map/reduce_scatter | solution.py:44
  238.8 133.6 %reduce-scatter.5.cloned.1.call-start = ((), (), s32[]{:S(2)}) async-start(), calls=%async_computation.6 | async-start | bytes 8912896 | tf_op jit(solution)/shard_map/reduce_scatter | solution.py:45
Sparse Core Ops, SparseCore 0:
  238.9 29.0 reduce-scatter.2
  270.6 101.8 reduce-scatter.4
